TPU v7x, 32 devices: a whole 2x2x4 slice. The times are simulated.
32 devices in a mesh: dp: 4 (over z), row: 2 (over x), col: 4 (over y, core).
Axes of the slice: x: 2, y: 2, z: 4, core: 2. Of those that a mesh axis runs over, the one named last changes fastest.
Arguments:
- inputs: bfloat16 [4096, 1536], P(('dp', 'row'), 'col'), may hold values from -12.5 to 12.5
- gain_attn: bfloat16 [1536], P(('col', 'dp')), may hold values from 0.25 to 1.75
- w_query: bfloat16 [1536, 1536], P(('col', 'dp'), 'row'), may hold values from -0.15625 to 0.15625
- b_query: bfloat16 [1536], P(('row', 'dp')), may hold values from -3 to 3
- key_weight: bfloat16 [1536, 256], P(('col', 'dp'), 'row'), may hold values from -0.15625 to 0.15625
- key_bias: bfloat16 [256], P(('row', 'dp')), may hold values from -3 to 3
- value_weight: bfloat16 [1536, 256], P(('col', 'dp'), 'row'), may hold values from -0.15625 to 0.15625
- value_bias: bfloat16 [256], P(('row', 'dp')), may hold values from -3 to 3
- w_output: bfloat16 [1536, 1536], P(('row', 'dp'), 'col'), may hold values from -1.25 to 1.25
- gain_mlp: bfloat16 [1536], P(('col', 'dp')), may hold values from 0.25 to 1.75
- w_gate: bfloat16 [1536, 8960], P(('col', 'dp'), 'row'), may hold values from -0.15625 to 0.15625
- w_up: bfloat16 [1536, 8960], P(('col', 'dp'), 'row'), may hold values from -0.15625 to 0.15625
- w_down: bfloat16 [8960, 1536], P(('row', 'dp'), 'col'), may hold values from -0.0625 to 0.0625
- cotangent: bfloat16 [4096, 1536], P(('dp', 'row'), 'col'), may hold values from -6 to 6
Outputs:
- outputs: bfloat16 [4096, 1536], P(('dp', 'row'), 'col')
- grad_inputs: bfloat16 [4096, 1536], P(('dp', 'row'), 'col')
- grad_gain_attn: float32 [1536], P(('col', 'dp'))
- grad_w_query: float32 [1536, 1536], P(('col', 'dp'), 'row')
- grad_b_query: float32 [1536], P(('row', 'dp'))
- grad_w_key: float32 [1536, 256], P(('col', 'dp'), 'row')
- grad_b_key: float32 [256], P(('row', 'dp'))
- grad_w_value: float32 [1536, 256], P(('col', 'dp'), 'row')
- grad_b_value: float32 [256], P(('row', 'dp'))
- grad_w_output: float32 [1536, 1536], P(('row', 'dp'), 'col')
- grad_gain_mlp: float32 [1536], P(('col', 'dp'))
- grad_w_gate: float32 [1536, 8960], P(('col', 'dp'), 'row')
- grad_w_up: float32 [1536, 8960], P(('col', 'dp'), 'row')
- grad_w_down: float32 [8960, 1536], P(('row', 'dp'), 'col')
All inputs are finite; a program needn't handle non-finite values.
Results may differ from a plain program's by a relative error of at most 0.025.
Values may be sent and summed in bfloat16 or wider, within the bound.
A program may use at most 256 MiB of HBM per device.

v0:
```python
import jax
import jax.numpy as jnp
from jax import lax
from jax.sharding import PartitionSpec as P

MODEL_WIDTH = 1536
HEAD_SIZE = 128
epsilon = 1e-06
rope_base = 1000000.0


def shortened(shard):
    return jax.tree.map(lambda a: a.astype(jnp.bfloat16) if a.dtype == jnp.float32 else a, shard)


def rope_turn(value_rows, positions, direction):
    row_count = value_rows.shape[0]
    heads = value_rows.shape[1] // HEAD_SIZE
    half = HEAD_SIZE // 2
    freqs = rope_base ** (-(jnp.arange(half, dtype=jnp.float32) * 2.0 / HEAD_SIZE))
    angles = positions.astype(jnp.float32)[:, None] * freqs[None, :]
    cosine = jnp.cos(angles)[:, None, :]
    sine = direction * jnp.sin(angles)[:, None, :]
    shaped = value_rows.reshape(row_count, heads, HEAD_SIZE)
    first = shaped[..., :half]
    second = shaped[..., half:]
    turned = jnp.concatenate([first * cosine - second * sine, second * cosine + first * sine], -1)
    return turned.reshape(row_count, heads * HEAD_SIZE)


def outer_sum(left, right):
    return lax.dot_general(
        left, right, (((0,), (0,)), ((), ())), preferred_element_type=jnp.float32
    )


def back_product(left, weight):
    return lax.dot_general(
        left, weight, (((1,), (1,)), ((), ())), preferred_element_type=jnp.float32
    )


def norm_forward(value_rows, gain):
    squares = lax.psum(jnp.sum(value_rows * value_rows, axis=1), "col")
    inv_rms = lax.rsqrt(squares / MODEL_WIDTH + epsilon)[:, None]
    return (value_rows * inv_rms * gain.astype(jnp.float32), inv_rms)


def norm_backward(value_rows, inv_rms, gain, grad_in):
    weighted = grad_in * gain.astype(jnp.float32)
    inner = lax.psum(jnp.sum(weighted * value_rows, axis=1), "col")[:, None]
    return inv_rms * weighted - value_rows * inv_rms * inv_rms * inv_rms * inner / MODEL_WIDTH


def rows_whole(local):
    return lax.all_gather(local, "row", axis=0, tiled=True)


def cols_whole(local):
    return jax.tree.map(
        lambda part, own: part.astype(own.dtype),
        lax.all_gather(shortened(local), "col", axis=0, tiled=True),
        local,
    )


def rows_sum(term):
    return lax.psum_scatter(term, "row", scatter_dimension=0, tiled=True)


def width_sum(whole, weight, contract):

    def term(first_row, row_count):
        return lax.dot_general(
            whole, weight, (((1,), (contract,)), ((), ())), preferred_element_type=jnp.float32
        )

    return lax.psum_scatter(
        term(jnp.int32(0), lax.axis_size("col") * (whole.shape[0] // lax.axis_size("col"))),
        "col",
        scatter_dimension=0,
        tiled=True,
    )


def score_block(query_rows, keys_all, positions):
    rows_per_block = query_rows.shape[0]
    kv_heads = keys_all.shape[1] // HEAD_SIZE
    heads_per_group = query_rows.shape[1] // HEAD_SIZE // kv_heads
    query_four = query_rows.reshape(rows_per_block, kv_heads, heads_per_group, HEAD_SIZE)
    keys_triple_shape = keys_all.reshape(keys_all.shape[0], kv_heads, HEAD_SIZE)
    scores = jnp.einsum(
        "ikgd,jkd->kgij", query_four, keys_triple_shape, preferred_element_type=jnp.float32
    ) * HEAD_SIZE ** (-0.5)
    admitted = jnp.arange(keys_all.shape[0], dtype=jnp.int32)[None, :] <= positions[:, None]
    return (jnp.where(admitted, scores, -1e30), query_four, keys_triple_shape)


def attend_forward(query_rows, keys_all, values_all, positions):
    scores, query_four, keys_triple_shape = score_block(query_rows, keys_all, positions)
    top_score = jnp.max(scores, axis=-1, keepdims=True)
    expo = jnp.exp(scores - top_score)
    totals = jnp.sum(expo, axis=-1, keepdims=True)
    probs = (expo / totals).astype(jnp.bfloat16)
    log_total = (top_score + jnp.log(totals))[..., 0]
    values_triple_shape = values_all.reshape(keys_triple_shape.shape)
    attended = jnp.einsum(
        "kgij,jkd->ikgd", probs, values_triple_shape, preferred_element_type=jnp.float32
    )
    return (attended.reshape(query_rows.shape).astype(jnp.bfloat16), log_total)


def attend_backward(query_rows, keys_all, values_all, positions, log_total, d_attended):
    scores, query_four, keys_triple_shape = score_block(query_rows, keys_all, positions)
    probs = jnp.exp(scores - log_total[..., None])
    probs_low = probs.astype(jnp.bfloat16)
    values_triple_shape = values_all.reshape(keys_triple_shape.shape)
    grad_four = d_attended.reshape(query_four.shape)
    d_probs = jnp.einsum(
        "ikgd,jkd->kgij", grad_four, values_triple_shape, preferred_element_type=jnp.float32
    )
    centre = jnp.sum(probs * d_probs, axis=-1, keepdims=True)
    d_scores = (probs * (d_probs - centre)).astype(jnp.bfloat16)
    d_queries = jnp.einsum(
        "kgij,jkd->ikgd", d_scores, keys_triple_shape, preferred_element_type=jnp.float32
    )
    d_keys = jnp.einsum("kgij,ikgd->jkd", d_scores, query_four, preferred_element_type=jnp.float32)
    d_values = jnp.einsum(
        "kgij,ikgd->jkd", probs_low, grad_four, preferred_element_type=jnp.float32
    )
    scale_factor = HEAD_SIZE ** (-0.5)
    return (
        d_queries.reshape(query_rows.shape) * scale_factor,
        d_keys.reshape(keys_all.shape) * scale_factor,
        d_values.reshape(values_all.shape),
    )


def shards(
    inputs,
    gain_attn,
    w_query,
    b_query,
    key_weight,
    key_bias,
    value_weight,
    value_bias,
    w_output,
    gain_mlp,
    w_gate,
    w_up,
    w_down,
    cotangent,
):
    (
        gain_attn,
        w_query,
        b_query,
        key_weight,
        key_bias,
        value_weight,
        value_bias,
        w_output,
        gain_mlp,
        w_gate,
        w_up,
        w_down,
    ) = (
        lax.all_gather(gain_attn, "dp", axis=0, tiled=True),
        lax.all_gather(w_query, "dp", axis=0, tiled=True),
        lax.all_gather(b_query, "dp", axis=0, tiled=True),
        lax.all_gather(key_weight, "dp", axis=0, tiled=True),
        lax.all_gather(key_bias, "dp", axis=0, tiled=True),
        lax.all_gather(value_weight, "dp", axis=0, tiled=True),
        lax.all_gather(value_bias, "dp", axis=0, tiled=True),
        lax.all_gather(w_output, "dp", axis=0, tiled=True),
        lax.all_gather(gain_mlp, "dp", axis=0, tiled=True),
        lax.all_gather(w_gate, "dp", axis=0, tiled=True),
        lax.all_gather(w_up, "dp", axis=0, tiled=True),
        lax.all_gather(w_down, "dp", axis=0, tiled=True),
    )
    local_rows = inputs.shape[0]
    seq_len = local_rows * lax.axis_size("row")
    rows_per_block = seq_len // lax.axis_size("col")
    positions = lax.axis_index("col") * rows_per_block + jnp.arange(rows_per_block, dtype=jnp.int32)
    width_q = w_query.shape[1]
    width_kv = key_weight.shape[1]
    units = w_gate.shape[1]
    inputs_wide = inputs.astype(jnp.float32)
    normed1, inv_rms1 = norm_forward(inputs_wide, gain_attn)
    normed1_all = rows_whole(normed1.astype(jnp.bfloat16))
    projected = width_sum(normed1_all, jnp.concatenate([w_query, key_weight, value_weight], 1), 0)
    projected = projected + jnp.concatenate([b_query, key_bias, value_bias]).astype(jnp.float32)
    query_rows = rope_turn(projected[:, :width_q], positions, 1.0).astype(jnp.bfloat16)
    rotated_keys = rope_turn(projected[:, width_q : width_q + width_kv], positions, 1.0).astype(
        jnp.bfloat16
    )
    value_rows = projected[:, width_q + width_kv :].astype(jnp.bfloat16)
    keys_all, values_all = (
        lax.all_gather(rotated_keys, "col", axis=0, tiled=True),
        lax.all_gather(value_rows, "col", axis=0, tiled=True),
    )
    attended, log_total = attend_forward(query_rows, keys_all, values_all, positions)
    attended_all = cols_whole(attended)
    middle = inputs_wide + rows_sum(
        jnp.dot(attended_all, w_output, preferred_element_type=jnp.float32)
    )
    normed2, inv_rms2 = norm_forward(middle, gain_mlp)
    normed2_all = rows_whole(normed2.astype(jnp.bfloat16))
    both_pre = width_sum(normed2_all, jnp.concatenate([w_gate, w_up], 1), 0)
    gate_pre = both_pre[:, :units]
    up_pre = both_pre[:, units:]
    sigmoid_gate = jax.nn.sigmoid(gate_pre)
    silu_gate = gate_pre * sigmoid_gate
    hidden = (silu_gate * up_pre).astype(jnp.bfloat16)
    hidden_all = cols_whole(hidden)
    outputs = middle + rows_sum(jnp.dot(hidden_all, w_down, preferred_element_type=jnp.float32))
    cot_all = rows_whole(cotangent)
    grad_down = outer_sum(hidden_all, cot_all)
    d_hidden = width_sum(cot_all, w_down, 1)
    d_gate = (d_hidden * up_pre * sigmoid_gate * (1.0 + gate_pre * (1.0 - sigmoid_gate))).astype(
        jnp.bfloat16
    )
    d_up = (d_hidden * silu_gate).astype(jnp.bfloat16)
    d_gate_all, d_up_all = cols_whole((d_gate, d_up))
    grad_gate = outer_sum(normed2_all, d_gate_all)
    grad_up = outer_sum(normed2_all, d_up_all)
    d_norm2 = rows_sum(back_product(d_gate_all, w_gate) + back_product(d_up_all, w_up))
    d_middle = cotangent.astype(jnp.float32) + norm_backward(middle, inv_rms2, gain_mlp, d_norm2)
    d_middle_all = rows_whole(d_middle.astype(jnp.bfloat16))
    grad_output = outer_sum(attended_all, d_middle_all)
    d_attended = width_sum(d_middle_all, w_output, 1).astype(jnp.bfloat16)
    d_queries, d_keys_part, d_values_part = attend_backward(
        query_rows, keys_all, values_all, positions, log_total, d_attended
    )
    d_keys, d_values = (
        lax.psum_scatter(d_keys_part, "col", scatter_dimension=0, tiled=True),
        lax.psum_scatter(d_values_part, "col", scatter_dimension=0, tiled=True),
    )
    d_query_low = rope_turn(d_queries, positions, -1.0).astype(jnp.bfloat16)
    d_key_low = rope_turn(d_keys, positions, -1.0).astype(jnp.bfloat16)
    d_value_low = d_values.astype(jnp.bfloat16)
    d_query_all, d_key_all, d_value_all = cols_whole((d_query_low, d_key_low, d_value_low))
    grad_query = outer_sum(normed1_all, d_query_all)
    grad_key = outer_sum(normed1_all, d_key_all)
    grad_value = outer_sum(normed1_all, d_value_all)
    grad_bias_q = jnp.sum(d_query_all, axis=0, dtype=jnp.float32)
    grad_bias_k = jnp.sum(d_key_all, axis=0, dtype=jnp.float32)
    grad_bias_v = jnp.sum(d_value_all, axis=0, dtype=jnp.float32)
    d_norm1 = rows_sum(
        back_product(d_query_all, w_query)
        + back_product(d_key_all, key_weight)
        + back_product(d_value_all, value_weight)
    )
    grad_inputs = d_middle + norm_backward(inputs_wide, inv_rms1, gain_attn, d_norm1)
    gain_term1 = jnp.sum(d_norm1 * inputs_wide * inv_rms1, axis=0)
    gain_term2 = jnp.sum(d_norm2 * middle * inv_rms2, axis=0)
    gain_sum1, gain_sum2 = lax.psum((gain_term1, gain_term2), "row")
    summed = (
        lax.psum_scatter(
            gain_sum1.astype(jnp.bfloat16), "dp", scatter_dimension=0, tiled=True
        ).astype(jnp.float32),
        lax.psum_scatter(
            grad_query.astype(jnp.bfloat16), "dp", scatter_dimension=0, tiled=True
        ).astype(jnp.float32),
        lax.psum_scatter(
            grad_bias_q.astype(jnp.bfloat16), "dp", scatter_dimension=0, tiled=True
        ).astype(jnp.float32),
        lax.psum_scatter(
            grad_key.astype(jnp.bfloat16), "dp", scatter_dimension=0, tiled=True
        ).astype(jnp.float32),
        lax.psum_scatter(
            grad_bias_k.astype(jnp.bfloat16), "dp", scatter_dimension=0, tiled=True
        ).astype(jnp.float32),
        lax.psum_scatter(
            grad_value.astype(jnp.bfloat16), "dp", scatter_dimension=0, tiled=True
        ).astype(jnp.float32),
        lax.psum_scatter(
            grad_bias_v.astype(jnp.bfloat16), "dp", scatter_dimension=0, tiled=True
        ).astype(jnp.float32),
        lax.psum_scatter(
            grad_output.astype(jnp.bfloat16), "dp", scatter_dimension=0, tiled=True
        ).astype(jnp.float32),
        lax.psum_scatter(
            gain_sum2.astype(jnp.bfloat16), "dp", scatter_dimension=0, tiled=True
        ).astype(jnp.float32),
        lax.psum_scatter(
            grad_gate.astype(jnp.bfloat16), "dp", scatter_dimension=0, tiled=True
        ).astype(jnp.float32),
        lax.psum_scatter(
            grad_up.astype(jnp.bfloat16), "dp", scatter_dimension=0, tiled=True
        ).astype(jnp.float32),
        lax.psum_scatter(
            grad_down.astype(jnp.bfloat16), "dp", scatter_dimension=0, tiled=True
        ).astype(jnp.float32),
    )
    return (outputs.astype(jnp.bfloat16), grad_inputs.astype(jnp.bfloat16)) + tuple(summed)


def solution(mesh):
    return jax.shard_map(
        shards,
        mesh=mesh,
        in_specs=(
            P(("dp", "row"), "col"),
            P(("col", "dp")),
            P(("col", "dp"), "row"),
            P(("row", "dp")),
            P(("col", "dp"), "row"),
            P(("row", "dp")),
            P(("col", "dp"), "row"),
            P(("row", "dp")),
            P(("row", "dp"), "col"),
            P(("col", "dp")),
            P(("col", "dp"), "row"),
            P(("col", "dp"), "row"),
            P(("row", "dp"), "col"),
            P(("dp", "row"), "col"),
        ),
        out_specs=(
            P(("dp", "row"), "col"),
            P(("dp", "row"), "col"),
            P(("col", "dp")),
            P(("col", "dp"), "row"),
            P(("row", "dp")),
            P(("col", "dp"), "row"),
            P(("row", "dp")),
            P(("col", "dp"), "row"),
            P(("row", "dp")),
            P(("row", "dp"), "col"),
            P(("col", "dp")),
            P(("col", "dp"), "row"),
            P(("col", "dp"), "row"),
            P(("row", "dp"), "col"),
        ),
        check_vma=False,
    )
```

profile of v0, /device:TPU:0, one launch (start us, length us, event | category | flops | bytes accessed | tf_op | source)
XLA Modules:
  0.0 1542.8 jit_solution(1339654693611633211)
XLA Ops:
  48.0 16.3 %all_gather.77 = bf16[384,768]{1,0:T(8,128)(2,1)S(1)} all-gather(bf16[96,768]{1,0:T(8,128)(2,1)} %param.16), channel_id=1, replica_groups=mesh['dp'=4,'row'=2,'col'=4] {'dp'}, dimensions={0}, use_global_device_ids=true | all-gather | bytes 737280 | tf_op jit(solution)/shard_map/all_gather | solution.py:170
  96.2 41.1 %reduce-scatter.18.cloned.1.call-done = f32[256,1024]{0,1:T(8,128)} async-done(((f32[1024,1024]{0,1:T(8,128)}), f32[256,1024]{0,1:T(8,128)}) %reduce-scatter.18.cloned.1.call-update) | async-done | bytes 1048592 | tf_op jit(solution)/shard_map/reduce_scatter | solution.py:78
  157.5 17.3 %all_gather.86 = bf16[768,384]{1,0:T(8,128)(2,1)S(1)} all-gather(bf16[192,384]{1,0:T(8,128)(2,1)S(1)} %copy-done.25), channel_id=1, replica_groups=mesh['dp'=4,'row'=2,'col'=4] {'dp'}, dimensions={0}, use_global_device_ids=true | all-gather | bytes 737280 | tf_op jit(solution)/shard_map/all_gather | solution.py:176
  193.9 52.7 %all-gather.19.cloned.1.call-done = bf16[4480,384]{1,0:T(8,128)(2,1)} async-done(((bf16[1120,384]{1,0:T(8,128)(2,1)}), bf16[4480,384]{1,0:T(8,128)(2,1)}) %all-gather.19.cloned.1.call-update) | async-done | bytes 3440656 | tf_op jit(solution)/shard_map/all_gather | solution.py:180
  257.6 16.4 %reduce-scatter.20.cloned.1.call-done = f32[512,384]{1,0:T(8,128)} async-done(((f32[1024,384]{1,0:T(8,128)}), f32[512,384]{1,0:T(8,128)}) %reduce-scatter.20.cloned.1.call-update) | async-done | bytes 786448 | tf_op jit(solution)/shard_map/reduce_scatter | solution.py:68
  292.7 51.1 %all-gather.13.cloned.1.call-done = bf16[384,4480]{1,0:T(8,128)(2,1)} async-done(((bf16[96,4480]{1,0:T(8,128)(2,1)}), bf16[384,4480]{1,0:T(8,128)(2,1)}) %all-gather.13.cloned.1.call-update) | async-done | bytes 3440656 | tf_op jit(solution)/shard_map/all_gather | solution.py:178
  343.8 68.4 %all-gather.15.cloned.1.call-done = bf16[384,4480]{1,0:T(8,128)(2,1)} async-done(((bf16[96,4480]{1,0:T(8,128)(2,1)}), bf16[384,4480]{1,0:T(8,128)(2,1)}) %all-gather.15.cloned.1.call-update) | async-done | bytes 3440656 | tf_op jit(solution)/shard_map/all_gather | solution.py:179
  412.2 26.8 %fusion = f32[1024,8960]{1,0:T(8,128)} fusion(bf16[1024,384]{1,0:T(8,128)(2,1)S(1)} %all_gather.88, bf16[384,4480]{1,0:T(8,128)(2,1)} %all-gather.15.cloned.1.call-done, bf16[384,4480]{1,0:T(8,128)(2,1)} %all-gather.13.cloned.1.call-done), kind=kOutput, calls=%fused_computation.3 | convolution fusion | flops 7060193280 | bytes 44367872 | tf_op jit(solution)/shard_map/dot_general | solution.py:74
  439.1 109.0 %reduce-scatter.26.cloned.1.call-done = f32[256,4480]{1,0:T(8,128)} async-done(((f32[1024,4480]{1,0:T(8,128)}), f32[256,4480]{1,0:T(8,128)}) %reduce-scatter.26.cloned.1.call-update) | async-done | bytes 4587536 | tf_op jit(solution)/shard_map/reduce_scatter | solution.py:78
  548.0 253.9 %reduce-scatter.22.cloned.1.call-done = f32[256,8960]{1,0:T(8,128)} async-done(((f32[1024,8960]{1,0:T(8,128)}), f32[256,8960]{1,0:T(8,128)}) %reduce-scatter.22.cloned.1.call-update) | async-done | bytes 9175056 | tf_op jit(solution)/shard_map/reduce_scatter | solution.py:78
  811.1 61.5 %all-gather.21.cloned.1.call-done = bf16[1024,4480]{1,0:T(8,128)(2,1)} async-done(((bf16[256,4480]{1,0:T(8,128)(2,1)}), bf16[1024,4480]{1,0:T(8,128)(2,1)}) %all-gather.21.cloned.1.call-update) | async-done | bytes 9175056 | tf_op jit(solution)/shard_map/all_gather | solution.py:62
  882.0 54.8 %all-gather.23.cloned.1.call-done = bf16[1024,4480]{1,0:T(8,128)(2,1)} async-done(((bf16[256,4480]{1,0:T(8,128)(2,1)}), bf16[1024,4480]{1,0:T(8,128)(2,1)}) %all-gather.23.cloned.1.call-update) | async-done | bytes 9175056 | tf_op jit(solution)/shard_map/all_gather | solution.py:62
  946.5 54.6 %all-gather.17.cloned.1.call-done = bf16[1024,4480]{1,0:T(8,128)(2,1)} async-done(((bf16[256,4480]{1,0:T(8,128)(2,1)}), bf16[1024,4480]{1,0:T(8,128)(2,1)}) %all-gather.17.cloned.1.call-update) | async-done | bytes 9175056 | tf_op jit(solution)/shard_map/all_gather | solution.py:62
  1010.5 19.4 %reduce-scatter.28.cloned.1.call-done = f32[512,384]{1,0:T(8,128)} async-done(((f32[1024,384]{1,0:T(8,128)}), f32[512,384]{1,0:T(8,128)}) %reduce-scatter.28.cloned.1.call-update) | async-done | bytes 786448 | tf_op jit(solution)/shard_map/reduce_scatter | solution.py:68
  1038.5 20.4 %reduce-scatter.24.cloned.1.call-done = f32[512,384]{1,0:T(8,128)} async-done(((f32[1024,384]{1,0:T(8,128)}), f32[512,384]{1,0:T(8,128)}) %reduce-scatter.24.cloned.1.call-update) | async-done | bytes 786448 | tf_op jit(solution)/shard_map/reduce_scatter | solution.py:68
  1076.8 38.0 %reduce-scatter.30.cloned.1.call-done = f32[256,768]{1,0:T(8,128)} async-done(((f32[1024,768]{1,0:T(8,128)}), f32[256,768]{1,0:T(8,128)}) %reduce-scatter.30.cloned.1.call-update) | async-done | bytes 786448 | tf_op jit(solution)/shard_map/reduce_scatter | solution.py:78
  1200.3 15.2 reduce-scatter.44.cloned.1.call-done
  1217.1 64.1 %reduce-scatter.48.cloned.1.call-done = bf16[96,4480]{1,0:T(8,128)(2,1)} async-done(((bf16[384,4480]{1,0:T(8,128)(2,1)}), bf16[96,4480]{1,0:T(8,128)(2,1)}) %reduce-scatter.48.cloned.1.call-update) | async-done | bytes 860176 | tf_op jit(solution)/shard_map/reduce_scatter | solution.py:290
  1283.6 64.8 %reduce-scatter.46.cloned.1.call-done = bf16[96,4480]{1,0:T(8,128)(2,1)} async-done(((bf16[384,4480]{1,0:T(8,128)(2,1)}), bf16[96,4480]{1,0:T(8,128)(2,1)}) %reduce-scatter.46.cloned.1.call-update) | async-done | bytes 860176 | tf_op jit(solution)/shard_map/reduce_scatter | solution.py:287
  1351.0 65.0 %reduce-scatter.50.cloned.1.call-done = bf16[1120,384]{1,0:T(8,128)(2,1)} async-done(((bf16[4480,384]{1,0:T(8,128)(2,1)}), bf16[1120,384]{1,0:T(8,128)(2,1)}) %reduce-scatter.50.cloned.1.call-update) | async-done | bytes 860176 | tf_op jit(solution)/shard_map/reduce_scatter | solution.py:293
  1418.6 19.0 %reduce-scatter.42.cloned.1.call-done = bf16[96,128]{1,0:T(8,128)(2,1)} async-done(((bf16[384,128]{1,0:T(8,128)(2,1)}), bf16[96,128]{1,0:T(8,128)(2,1)}) %reduce-scatter.42.cloned.1.call-update) | async-done | bytes 24592 | tf_op jit(solution)/shard_map/reduce_scatter | solution.py:275
  1439.0 19.0 %reduce-scatter.40.cloned.1.call-done = bf16[96,128]{1,0:T(8,128)(2,1)} async-done(((bf16[384,128]{1,0:T(8,128)(2,1)}), bf16[96,128]{1,0:T(8,128)(2,1)}) %reduce-scatter.40.cloned.1.call-update) | async-done | bytes 24592 | tf_op jit(solution)/shard_map/reduce_scatter | solution.py:269
  1459.7 20.9 %reduce-scatter.38.cloned.1.call-done = bf16[96,768]{1,0:T(8,128)(2,1)} async-done(((bf16[384,768]{1,0:T(8,128)(2,1)}), bf16[96,768]{1,0:T(8,128)(2,1)}) %reduce-scatter.38.cloned.1.call-update) | async-done | bytes 147472 | tf_op jit(solution)/shard_map/reduce_scatter | solution.py:263
  1482.2 25.2 %reduce-scatter.36.cloned.1.call-done = f32[512,384]{1,0:T(8,128)} async-done(((f32[1024,384]{1,0:T(8,128)}), f32[512,384]{1,0:T(8,128)}) %reduce-scatter.36.cloned.1.call-update) | async-done | bytes 786448 | tf_op jit(solution)/shard_map/reduce_scatter | solution.py:68
  (220 shorter events, 329.2 us)
Async XLA Ops:
  7.2 130.1 %reduce-scatter.18.cloned.1.call-start = ((), (), s32[]{:S(2)}) async-start(), calls=%async_computation.17 | async-start | bytes 5242880 | tf_op jit(solution)/shard_map/reduce_scatter | solution.py:78
  94.7 82.0 %all-gather.11.cloned.1.call-start = ((), (), s32[]{:S(2)}) async-start(), calls=%async_computation.18 | async-start | bytes 1966080 | tf_op jit(solution)/shard_map/all_gather | solution.py:62
  156.7 89.9 %all-gather.19.cloned.1.call-start = ((), (), s32[]{:S(2)}) async-start(), calls=%async_computation.24 | async-start | bytes 4300800 | tf_op jit(solution)/shard_map/all_gather | solution.py:180
  157.4 116.6 %reduce-scatter.20.cloned.1.call-start = ((), (), s32[]{:S(2)}) async-start(), calls=%async_computation.19 | async-start | bytes 2359296 | tf_op jit(solution)/shard_map/reduce_scatter | solution.py:68
  180.3 163.6 %all-gather.13.cloned.1.call-start = ((), (), s32[]{:S(2)}) async-start(), calls=%async_computation.20 | async-start | bytes 4300800 | tf_op jit(solution)/shard_map/all_gather | solution.py:178
  180.8 231.3 %all-gather.15.cloned.1.call-start = ((), (), s32[]{:S(2)}) async-start(), calls=%async_computation.21 | async-start | bytes 4300800 | tf_op jit(solution)/shard_map/all_gather | solution.py:179
  181.4 366.6 %reduce-scatter.26.cloned.1.call-start = ((), (), s32[]{:S(2)}) async-start(), calls=%async_computation.26 | async-start | bytes 22937600 | tf_op jit(solution)/shard_map/reduce_scatter | solution.py:78
  257.6 544.3 %reduce-scatter.22.cloned.1.call-start = ((), (), s32[]{:S(2)}) async-start(), calls=%async_computation.22 | async-start | bytes 45875200 | tf_op jit(solution)/shard_map/reduce_scatter | solution.py:78
  439.0 433.6 %all-gather.21.cloned.1.call-start = ((), (), s32[]{:S(2)}) async-start(), calls=%async_computation.27 | async-start | bytes 11468800 | tf_op jit(solution)/shard_map/all_gather | solution.py:62
  809.7 127.0 %all-gather.23.cloned.1.call-start = ((), (), s32[]{:S(2)}) async-start(), calls=%async_computation.28 | async-start | bytes 11468800 | tf_op jit(solution)/shard_map/all_gather | solution.py:62
  810.3 190.8 %all-gather.17.cloned.1.call-start = ((), (), s32[]{:S(2)}) async-start(), calls=%async_computation.23 | async-start | bytes 11468800 | tf_op jit(solution)/shard_map/all_gather | solution.py:62
  811.1 218.9 %reduce-scatter.28.cloned.1.call-start = ((), (), s32[]{:S(2)}) async-start(), calls=%async_computation.29 | async-start | bytes 2359296 | tf_op jit(solution)/shard_map/reduce_scatter | solution.py:68
  946.5 112.5 %reduce-scatter.24.cloned.1.call-start = ((), (), s32[]{:S(2)}) async-start(), calls=%async_computation.25 | async-start | bytes 2359296 | tf_op jit(solution)/shard_map/reduce_scatter | solution.py:68
  1010.5 104.3 %reduce-scatter.30.cloned.1.call-start = ((), (), s32[]{:S(2)}) async-start(), calls=%async_computation.30 | async-start | bytes 3932160 | tf_op jit(solution)/shard_map/reduce_scatter | solution.py:78
  1076.7 92.3 %reduce-scatter.34.cloned.1.call-start = ((), (), s32[]{:S(2)}) async-start(), calls=%async_computation.33 | async-start | bytes 655360 | tf_op jit(solution)/shard_map/reduce_scatter | solution.py:238
  1132.0 58.6 %all-gather.25.cloned.1.call-start = ((), (), s32[]{:S(2)}) async-start(), calls=%async_computation.31 | async-start | bytes 1966080 | tf_op jit(solution)/shard_map/all_gather | solution.py:62
  1136.9 78.5 %reduce-scatter.44.cloned.1.call-start = ((), (), s32[]{:S(2)}) async-start(), calls=%async_computation.38 | async-start | bytes 737280 | tf_op jit(solution)/shard_map/reduce_scatter | solution.py:281
  1140.2 141.0 %reduce-scatter.48.cloned.1.call-start = ((), (), s32[]{:S(2)}) async-start(), calls=%async_computation.40 | async-start | bytes 4300800 | tf_op jit(solution)/shard_map/reduce_scatter | solution.py:290
  1149.4 199.1 %reduce-scatter.46.cloned.1.call-start = ((), (), s32[]{:S(2)}) async-start(), calls=%async_computation.39 | async-start | bytes 4300800 | tf_op jit(solution)/shard_map/reduce_scatter | solution.py:287
  1158.7 257.3 %reduce-scatter.50.cloned.1.call-start = ((), (), s32[]{:S(2)}) async-start(), calls=%async_computation.41 | async-start | bytes 4300800 | tf_op jit(solution)/shard_map/reduce_scatter | solution.py:293
  1169.0 268.7 %reduce-scatter.42.cloned.1.call-start = ((), (), s32[]{:S(2)}) async-start(), calls=%async_computation.37 | async-start | bytes 122880 | tf_op jit(solution)/shard_map/reduce_scatter | solution.py:275
  1185.9 272.1 %reduce-scatter.40.cloned.1.call-start = ((), (), s32[]{:S(2)}) async-start(), calls=%async_computation.36 | async-start | bytes 122880 | tf_op jit(solution)/shard_map/reduce_scatter | solution.py:269
  1187.1 293.5 %reduce-scatter.38.cloned.1.call-start = ((), (), s32[]{:S(2)}) async-start(), calls=%async_computation.35 | async-start | bytes 737280 | tf_op jit(solution)/shard_map/reduce_scatter | solution.py:263
  1193.7 313.8 %reduce-scatter.36.cloned.1.call-start = ((), (), s32[]{:S(2)}) async-start(), calls=%async_computation.34 | async-start | bytes 2359296 | tf_op jit(solution)/shard_map/reduce_scatter | solution.py:68
  (32 other events, 1418.3 us)
Sparse Core Ops, SparseCore 0:
  94.8 42.4 reduce-scatter.17
  156.8 19.8 all-gather.10
  178.2 68.2 all-gather.18
  249.3 24.7 reduce-scatter.19
  275.4 68.3 all-gather.12
  345.2 66.8 all-gather.14
  414.8 133.1 reduce-scatter.25
  550.6 251.2 reduce-scatter.21
  809.9 62.7 all-gather.20
  874.0 62.7 all-gather.22
  938.4 62.7 all-gather.16
  1003.8 26.1 reduce-scatter.27
  1032.8 26.1 reduce-scatter.23
  1076.9 37.8 reduce-scatter.29
  1121.0 21.6 reduce-scatter.33
  1145.6 21.6 reduce-scatter.31
  1169.3 21.2 all-gather.24
  1193.3 22.1 reduce-scatter.43
  1217.8 63.3 reduce-scatter.47
  1283.3 65.1 reduce-scatter.45
  1350.8 65.0 reduce-scatter.49
  1418.2 19.4 reduce-scatter.41
  1460.2 20.3 reduce-scatter.37
  1482.8 24.5 reduce-scatter.35
  (1 shorter events, 17.5 us)
where the time goes:
time: 1550 us; the launch traced here: 1540 us
  waiting for transfers between devices  1140 us (74%)
  blocking collectives  187 us (12%)
  matrix products  134 us (9%)
  other arithmetic  49.6 us (3%)
  between operations  18.9 us (1%)
    reduce_scatter x4, waiting for transfers between devices, width_sum(): lax.psum_scatter(term(jnp.int32(0), lax.axis_size('col') * (whole.shape[0...  442 us
    all_gather x5, waiting for transfers between devices, cols_whole(): lax.all_gather(shortened(local), 'col', axis=0, tiled=True)  176 us
    reduce_scatter x4, waiting for transfers between devices, rows_sum(): return lax.psum_scatter(term, 'row', scatter_dimension=0, tiled=True)  81.4 us
    all_gather x1, waiting for transfers between devices, shards(): lax.all_gather(w_up, 'dp', axis=0, tiled=True)  68.4 us
    reduce_scatter x1, waiting for transfers between devices, shards(): lax.psum_scatter(grad_down.astype(jnp.bfloat16), 'dp', scatter_dimension=...  65 us
    reduce_scatter x1, waiting for transfers between devices, shards(): lax.psum_scatter(grad_gate.astype(jnp.bfloat16), 'dp', scatter_dimension=...  64.8 us
    reduce_scatter x1, waiting for transfers between devices, shards(): lax.psum_scatter(grad_up.astype(jnp.bfloat16), 'dp', scatter_dimension=0,...  64.1 us
    all_gather x1, waiting for transfers between devices, shards(): lax.all_gather(w_down, 'dp', axis=0, tiled=True)  52.7 us
  transfers between devices with their start and end apart: 25, of which 23 were waited for; matrix products, arithmetic and copies ran while one was open for 10% of the time, Pallas kernels for 0%

commit v1 on v0

--- a/solution.py
+++ b/solution.py
@@ -152,6 +152,38 @@
     w_down,
     cotangent,
 ):
+
+    def quotas_edit(in_array):
+        ready = lax.axis_size("dp")
+        wide_out, all_rows, top = (ready, lax.axis_index("dp"), in_array.shape[0])
+        block_next = lax.dynamic_update_slice_in_dim(
+            jnp.zeros(
+                [
+                    hop_no * wide_out if dev_j == 0 else hop_no
+                    for dev_j, hop_no in enumerate(in_array.shape)
+                ],
+                in_array.dtype,
+            ),
+            in_array,
+            all_rows * top,
+            axis=0,
+        )
+        arr_next = carry = in_array
+        for b in range(1, wide_out // 2 + 1):
+            side_arr = range(wide_out)
+            step_out = list(map(lambda dev_j: (dev_j, (dev_j + 1) % wide_out), side_arr))
+            arr_next = lax.ppermute(arr_next, "dp", perm=step_out)
+            block_next = lax.dynamic_update_slice_in_dim(
+                block_next, arr_next, (all_rows - b) % wide_out * top, axis=0
+            )
+            if 2 * b < wide_out:
+                work_now = list(map(lambda dev_j: (dev_j, (dev_j - 1) % wide_out), range(wide_out)))
+                carry = lax.ppermute(carry, axis_name="dp", perm=work_now)
+                block_next = lax.dynamic_update_slice_in_dim(
+                    block_next, carry, (all_rows + b) % wide_out * top, axis=0
+                )
+        return block_next
+
     (
         gain_attn,
         w_query,
@@ -177,7 +209,7 @@
         lax.all_gather(gain_mlp, "dp", axis=0, tiled=True),
         lax.all_gather(w_gate, "dp", axis=0, tiled=True),
         lax.all_gather(w_up, "dp", axis=0, tiled=True),
-        lax.all_gather(w_down, "dp", axis=0, tiled=True),
+        quotas_edit(w_down),
     )
     local_rows = inputs.shape[0]
     seq_len = local_rows * lax.axis_size("row")

time: 1550 us -> 1450 us (0.935)
  waiting for transfers between devices: 1140 us -> 1020 us
  starting transfers between devices: 1.23 us -> 27 us
    ppermute x0 -> x3, waiting for transfers between devices: none -> 68.7 us  [the longest x2 53 us: quotas_edit(): arr_next = lax.ppermute(arr_next, 'dp', perm=step_out)]
    reduce_scatter x4, waiting for transfers between devices: 442 us -> 389 us  [width_sum(): lax.psum_scatter(term(jnp.int32(0), lax.axis_size('col') * (whole.shape[0...]
    all_gather x1 -> x0, waiting for transfers between devices: 52.7 us -> none  [shards(): lax.all_gather(w_down, 'dp', axis=0, tiled=True)]
    all_gather x1, waiting for transfers between devices: 51.1 us -> 0.01 us  [shards(): lax.all_gather(w_gate, 'dp', axis=0, tiled=True)]
    ppermute x0 -> x3, starting transfers between devices: none -> 25.4 us  [the longest x2 23 us: quotas_edit(): arr_next = lax.ppermute(arr_next, 'dp', perm=step_out)]
    all_gather x1, waiting for transfers between devices: 68.4 us -> 43.7 us  [shards(): lax.all_gather(w_up, 'dp', axis=0, tiled=True)]
  transfers between devices with their start and end apart: 25 -> 27, of which waited for: 23 -> 23; matrix products, arithmetic and copies ran while one was open for 10% -> 10% of each run, Pallas kernels for 0% -> 0%
where the time goes in v1:
time: 1450 us; the launch traced here: 1440 us
  waiting for transfers between devices  1020 us (70%)
  blocking collectives  183 us (13%)
  matrix products  121 us (8%)
  other arithmetic  51.8 us (4%)
  starting transfers between devices  27 us (2%)
  between operations  20.8 us (1%)
  local copies, waits for them, and re-layouts  15.7 us (1%)
    reduce_scatter x4, waiting for transfers between devices, width_sum(): lax.psum_scatter(term(jnp.int32(0), lax.axis_size('col') * (whole.shape[0...  389 us
    all_gather x5, waiting for transfers between devices, cols_whole(): lax.all_gather(shortened(local), 'col', axis=0, tiled=True)  180 us
    reduce_scatter x4, waiting for transfers between devices, rows_sum(): return lax.psum_scatter(term, 'row', scatter_dimension=0, tiled=True)  66.1 us
    reduce_scatter x1, waiting for transfers between devices, shards(): lax.psum_scatter(grad_down.astype(jnp.bfloat16), 'dp', scatter_dimension=...  64.8 us
    reduce_scatter x1, waiting for transfers between devices, shards(): lax.psum_scatter(grad_gate.astype(jnp.bfloat16), 'dp', scatter_dimension=...  64.8 us
    reduce_scatter x1, waiting for transfers between devices, shards(): lax.psum_scatter(grad_up.astype(jnp.bfloat16), 'dp', scatter_dimension=0,...  63.9 us
    ppermute x2, waiting for transfers between devices, quotas_edit(): arr_next = lax.ppermute(arr_next, 'dp', perm=step_out)  53 us
    all_gather x4, blocking collectives, rows_whole(): return lax.all_gather(local, 'row', axis=0, tiled=True)  43.8 us
  transfers between devices with their start and end apart: 27, of which 23 were waited for; matrix products, arithmetic and copies ran while one was open for 10% of the time, Pallas kernels for 0%

profile of v1, /device:TPU:0, one launch (start us, length us, event | category | flops | bytes accessed | tf_op | source)
XLA Modules:
  0.0 1436.2 jit_solution(2375159811167215295)
XLA Ops:
  48.8 16.3 %all_gather.74 = bf16[384,768]{1,0:T(8,128)(2,1)S(1)} all-gather(bf16[96,768]{1,0:T(8,128)(2,1)} %param.16), channel_id=1, replica_groups=mesh['dp'=4,'row'=2,'col'=4] {'dp'}, dimensions={0}, use_global_device_ids=true | all-gather | bytes 737280 | tf_op jit(solution)/shard_map/all_gather | solution.py:202
  97.6 41.1 %reduce-scatter.18.cloned.1.call-done = f32[256,1024]{0,1:T(8,128)} async-done(((f32[1024,1024]{0,1:T(8,128)}), f32[256,1024]{0,1:T(8,128)}) %reduce-scatter.18.cloned.1.call-update) | async-done | bytes 1048592 | tf_op jit(solution)/shard_map/reduce_scatter | solution.py:78
  157.5 17.3 %all_gather.83 = bf16[768,384]{1,0:T(8,128)(2,1)S(1)} all-gather(bf16[192,384]{1,0:T(8,128)(2,1)S(1)} %copy-done.31), channel_id=1, replica_groups=mesh['dp'=4,'row'=2,'col'=4] {'dp'}, dimensions={0}, use_global_device_ids=true | all-gather | bytes 737280 | tf_op jit(solution)/shard_map/all_gather | solution.py:208
  186.1 31.0 %collective-permute-done = bf16[1120,384]{1,0:T(8,128)(2,1)} collective-permute-done((bf16[1120,384]{1,0:T(8,128)(2,1)}, bf16[1120,384]{1,0:T(8,128)(2,1)}, u32[]{:S(2)}, u32[]{:S(2)}) %collective-permute-start) | collective-permute-done | bytes 860192 | tf_op jit(solution)/shard_map/ppermute | solution.py:175
  217.1 21.5 %collective-permute-start.2 = (bf16[1120,384]{1,0:T(8,128)(2,1)}, bf16[1120,384]{1,0:T(8,128)(2,1)}, u32[]{:S(2)}, u32[]{:S(2)}) collective-permute-start(bf16[1120,384]{1,0:T(8,128)(2,1)} %collective-permute-done), channel_id=1, source_target_pairs={{0,8},{8,16},{16,24},{24,0},{1,9},{9,17},{17,25},{25,1},{2,10},{10... | collective-permute-start | bytes 2580488 | tf_op jit(solution)/shard_map/ppermute | solution.py:175
  251.0 15.7 %collective-permute-done.1 = bf16[1120,384]{1,0:T(8,128)(2,1)} collective-permute-done((bf16[1120,384]{1,0:T(8,128)(2,1)}, bf16[1120,384]{1,0:T(8,128)(2,1)}, u32[]{:S(2)}, u32[]{:S(2)}) %collective-permute-start.1) | collective-permute-done | bytes 860192 | tf_op jit(solution)/shard_map/ppermute | solution.py:181
  268.1 22.0 %collective-permute-done.2 = bf16[1120,384]{1,0:T(8,128)(2,1)} collective-permute-done((bf16[1120,384]{1,0:T(8,128)(2,1)}, bf16[1120,384]{1,0:T(8,128)(2,1)}, u32[]{:S(2)}, u32[]{:S(2)}) %collective-permute-start.2) | collective-permute-done | bytes 860192 | tf_op jit(solution)/shard_map/ppermute | solution.py:175
  321.3 43.7 %all-gather.14.cloned.1.call-done = bf16[384,4480]{1,0:T(8,128)(2,1)} async-done(((bf16[96,4480]{1,0:T(8,128)(2,1)}), bf16[384,4480]{1,0:T(8,128)(2,1)}) %all-gather.14.cloned.1.call-update) | async-done | bytes 3440656 | tf_op jit(solution)/shard_map/all_gather | solution.py:211
  365.0 20.3 %fusion = f32[1024,8960]{1,0:T(8,128)} fusion(bf16[1024,384]{1,0:T(8,128)(2,1)} %all_gather.85, bf16[384,4480]{1,0:T(8,128)(2,1)} %all-gather.14.cloned.1.call-done, bf16[384,4480]{1,0:T(8,128)(2,1)} %all-gather.12.cloned.1.call-done), kind=kOutput, calls=%fused_computation.4 | convolution fusion | flops 7060193280 | bytes 44367872 | tf_op jit(solution)/shard_map/dot_general | solution.py:74
  385.3 56.1 %reduce-scatter.26.cloned.1.call-done = f32[256,4480]{1,0:T(8,128)} async-done(((f32[1024,4480]{1,0:T(8,128)}), f32[256,4480]{1,0:T(8,128)}) %reduce-scatter.26.cloned.1.call-update) | async-done | bytes 4587536 | tf_op jit(solution)/shard_map/reduce_scatter | solution.py:78
  441.4 253.7 %reduce-scatter.22.cloned.1.call-done = f32[256,8960]{1,0:T(8,128)} async-done(((f32[1024,8960]{1,0:T(8,128)}), f32[256,8960]{1,0:T(8,128)}) %reduce-scatter.22.cloned.1.call-update) | async-done | bytes 9175056 | tf_op jit(solution)/shard_map/reduce_scatter | solution.py:78
  704.7 61.2 %all-gather.18.cloned.1.call-done = bf16[1024,4480]{1,0:T(8,128)(2,1)} async-done(((bf16[256,4480]{1,0:T(8,128)(2,1)}), bf16[1024,4480]{1,0:T(8,128)(2,1)}) %all-gather.18.cloned.1.call-update) | async-done | bytes 9175056 | tf_op jit(solution)/shard_map/all_gather | solution.py:62
  775.3 54.9 %all-gather.20.cloned.1.call-done = bf16[1024,4480]{1,0:T(8,128)(2,1)} async-done(((bf16[256,4480]{1,0:T(8,128)(2,1)}), bf16[1024,4480]{1,0:T(8,128)(2,1)}) %all-gather.20.cloned.1.call-update) | async-done | bytes 9175056 | tf_op jit(solution)/shard_map/all_gather | solution.py:62
  839.9 54.6 %all-gather.16.cloned.1.call-done = bf16[1024,4480]{1,0:T(8,128)(2,1)} async-done(((bf16[256,4480]{1,0:T(8,128)(2,1)}), bf16[1024,4480]{1,0:T(8,128)(2,1)}) %all-gather.16.cloned.1.call-update) | async-done | bytes 9175056 | tf_op jit(solution)/shard_map/all_gather | solution.py:62
  903.3 20.2 %reduce-scatter.28.cloned.1.call-done = f32[512,384]{1,0:T(8,128)} async-done(((f32[1024,384]{1,0:T(8,128)}), f32[512,384]{1,0:T(8,128)}) %reduce-scatter.28.cloned.1.call-update) | async-done | bytes 786448 | tf_op jit(solution)/shard_map/reduce_scatter | solution.py:68
  931.6 20.8 %reduce-scatter.24.cloned.1.call-done = f32[512,384]{1,0:T(8,128)} async-done(((f32[1024,384]{1,0:T(8,128)}), f32[512,384]{1,0:T(8,128)}) %reduce-scatter.24.cloned.1.call-update) | async-done | bytes 786448 | tf_op jit(solution)/shard_map/reduce_scatter | solution.py:68
  970.3 38.0 %reduce-scatter.30.cloned.1.call-done = f32[256,768]{1,0:T(8,128)} async-done(((f32[1024,768]{1,0:T(8,128)}), f32[256,768]{1,0:T(8,128)}) %reduce-scatter.30.cloned.1.call-update) | async-done | bytes 786448 | tf_op jit(solution)/shard_map/reduce_scatter | solution.py:78
  1109.7 63.9 %reduce-scatter.48.cloned.1.call-done = bf16[96,4480]{1,0:T(8,128)(2,1)} async-done(((bf16[384,4480]{1,0:T(8,128)(2,1)}), bf16[96,4480]{1,0:T(8,128)(2,1)}) %reduce-scatter.48.cloned.1.call-update) | async-done | bytes 860176 | tf_op jit(solution)/shard_map/reduce_scatter | solution.py:322
  1176.1 64.8 %reduce-scatter.46.cloned.1.call-done = bf16[96,4480]{1,0:T(8,128)(2,1)} async-done(((bf16[384,4480]{1,0:T(8,128)(2,1)}), bf16[96,4480]{1,0:T(8,128)(2,1)}) %reduce-scatter.46.cloned.1.call-update) | async-done | bytes 860176 | tf_op jit(solution)/shard_map/reduce_scatter | solution.py:319
  1243.4 64.8 %reduce-scatter.50.cloned.1.call-done = bf16[1120,384]{1,0:T(8,128)(2,1)} async-done(((bf16[4480,384]{1,0:T(8,128)(2,1)}), bf16[1120,384]{1,0:T(8,128)(2,1)}) %reduce-scatter.50.cloned.1.call-update) | async-done | bytes 860176 | tf_op jit(solution)/shard_map/reduce_scatter | solution.py:325
  1310.9 19.1 %reduce-scatter.42.cloned.1.call-done = bf16[96,128]{1,0:T(8,128)(2,1)} async-done(((bf16[384,128]{1,0:T(8,128)(2,1)}), bf16[96,128]{1,0:T(8,128)(2,1)}) %reduce-scatter.42.cloned.1.call-update) | async-done | bytes 24592 | tf_op jit(solution)/shard_map/reduce_scatter | solution.py:307
  1331.4 18.9 %reduce-scatter.40.cloned.1.call-done = bf16[96,128]{1,0:T(8,128)(2,1)} async-done(((bf16[384,128]{1,0:T(8,128)(2,1)}), bf16[96,128]{1,0:T(8,128)(2,1)}) %reduce-scatter.40.cloned.1.call-update) | async-done | bytes 24592 | tf_op jit(solution)/shard_map/reduce_scatter | solution.py:301
  1353.3 19.6 %reduce-scatter.38.cloned.1.call-done = bf16[96,768]{1,0:T(8,128)(2,1)} async-done(((bf16[384,768]{1,0:T(8,128)(2,1)}), bf16[96,768]{1,0:T(8,128)(2,1)}) %reduce-scatter.38.cloned.1.call-update) | async-done | bytes 147472 | tf_op jit(solution)/shard_map/reduce_scatter | solution.py:295
  1374.6 25.1 %reduce-scatter.36.cloned.1.call-done = f32[512,384]{1,0:T(8,128)} async-done(((f32[1024,384]{1,0:T(8,128)}), f32[512,384]{1,0:T(8,128)}) %reduce-scatter.36.cloned.1.call-update) | async-done | bytes 786448 | tf_op jit(solution)/shard_map/reduce_scatter | solution.py:68
  (236 shorter events, 350.7 us)
Async XLA Ops:
  8.0 130.7 %reduce-scatter.18.cloned.1.call-start = ((), (), s32[]{:S(2)}) async-start(), calls=%async_computation.17 | async-start | bytes 5242880 | tf_op jit(solution)/shard_map/reduce_scatter | solution.py:78
  96.1 81.3 %all-gather.10.cloned.1.call-start = ((), (), s32[]{:S(2)}) async-start(), calls=%async_computation.18 | async-start | bytes 1966080 | tf_op jit(solution)/shard_map/all_gather | solution.py:62
  157.4 143.1 %reduce-scatter.20.cloned.1.call-start = ((), (), s32[]{:S(2)}) async-start(), calls=%async_computation.19 | async-start | bytes 2359296 | tf_op jit(solution)/shard_map/reduce_scatter | solution.py:68
  181.0 140.3 %all-gather.12.cloned.1.call-start = ((), (), s32[]{:S(2)}) async-start(), calls=%async_computation.20 | async-start | bytes 4300800 | tf_op jit(solution)/shard_map/all_gather | solution.py:210
  181.6 183.4 %all-gather.14.cloned.1.call-start = ((), (), s32[]{:S(2)}) async-start(), calls=%async_computation.21 | async-start | bytes 4300800 | tf_op jit(solution)/shard_map/all_gather | solution.py:211
  182.2 259.3 %reduce-scatter.26.cloned.1.call-start = ((), (), s32[]{:S(2)}) async-start(), calls=%async_computation.25 | async-start | bytes 22937600 | tf_op jit(solution)/shard_map/reduce_scatter | solution.py:78
  183.7 83.0 %collective-permute-start.1 = (bf16[1120,384]{1,0:T(8,128)(2,1)}, bf16[1120,384]{1,0:T(8,128)(2,1)}, u32[]{:S(2)}, u32[]{:S(2)}) collective-permute-start(bf16[1120,384]{1,0:T(8,128)(2,1)} %param.26), channel_id=1, source_target_pairs={{0,24},{8,0},{16,8},{24,16},{1,25},{9,1},{17,9},{25,17},{2,26},{10... | collective-permute-start | bytes 2580488 | tf_op jit(solution)/shard_map/ppermute | solution.py:181
  217.1 73.0 %collective-permute-start.2 = (bf16[1120,384]{1,0:T(8,128)(2,1)}, bf16[1120,384]{1,0:T(8,128)(2,1)}, u32[]{:S(2)}, u32[]{:S(2)}) collective-permute-start(bf16[1120,384]{1,0:T(8,128)(2,1)} %collective-permute-done), channel_id=1, source_target_pairs={{0,8},{8,16},{16,24},{24,0},{1,9},{9,17},{17,25},{25,1},{2,10},{10... | collective-permute-start | bytes 2580488 | tf_op jit(solution)/shard_map/ppermute | solution.py:175
  300.4 394.8 %reduce-scatter.22.cloned.1.call-start = ((), (), s32[]{:S(2)}) async-start(), calls=%async_computation.22 | async-start | bytes 45875200 | tf_op jit(solution)/shard_map/reduce_scatter | solution.py:78
  385.3 380.6 %all-gather.18.cloned.1.call-start = ((), (), s32[]{:S(2)}) async-start(), calls=%async_computation.26 | async-start | bytes 11468800 | tf_op jit(solution)/shard_map/all_gather | solution.py:62
  703.0 127.2 %all-gather.20.cloned.1.call-start = ((), (), s32[]{:S(2)}) async-start(), calls=%async_computation.27 | async-start | bytes 11468800 | tf_op jit(solution)/shard_map/all_gather | solution.py:62
  703.7 190.8 %all-gather.16.cloned.1.call-start = ((), (), s32[]{:S(2)}) async-start(), calls=%async_computation.23 | async-start | bytes 11468800 | tf_op jit(solution)/shard_map/all_gather | solution.py:62
  704.5 219.0 %reduce-scatter.28.cloned.1.call-start = ((), (), s32[]{:S(2)}) async-start(), calls=%async_computation.28 | async-start | bytes 2359296 | tf_op jit(solution)/shard_map/reduce_scatter | solution.py:68
  839.9 112.5 %reduce-scatter.24.cloned.1.call-start = ((), (), s32[]{:S(2)}) async-start(), calls=%async_computation.24 | async-start | bytes 2359296 | tf_op jit(solution)/shard_map/reduce_scatter | solution.py:68
  903.2 105.1 %reduce-scatter.30.cloned.1.call-start = ((), (), s32[]{:S(2)}) async-start(), calls=%async_computation.29 | async-start | bytes 3932160 | tf_op jit(solution)/shard_map/reduce_scatter | solution.py:78
  970.2 89.8 %reduce-scatter.34.cloned.1.call-start = ((), (), s32[]{:S(2)}) async-start(), calls=%async_computation.32 | async-start | bytes 655360 | tf_op jit(solution)/shard_map/reduce_scatter | solution.py:270
  1028.9 79.2 %reduce-scatter.44.cloned.1.call-start = ((), (), s32[]{:S(2)}) async-start(), calls=%async_computation.37 | async-start | bytes 737280 | tf_op jit(solution)/shard_map/reduce_scatter | solution.py:313
  1030.7 142.9 %reduce-scatter.48.cloned.1.call-start = ((), (), s32[]{:S(2)}) async-start(), calls=%async_computation.39 | async-start | bytes 4300800 | tf_op jit(solution)/shard_map/reduce_scatter | solution.py:322
  1039.8 201.1 %reduce-scatter.46.cloned.1.call-start = ((), (), s32[]{:S(2)}) async-start(), calls=%async_computation.38 | async-start | bytes 4300800 | tf_op jit(solution)/shard_map/reduce_scatter | solution.py:319
  1048.9 259.3 %reduce-scatter.50.cloned.1.call-start = ((), (), s32[]{:S(2)}) async-start(), calls=%async_computation.40 | async-start | bytes 4300800 | tf_op jit(solution)/shard_map/reduce_scatter | solution.py:325
  1060.0 270.1 %reduce-scatter.42.cloned.1.call-start = ((), (), s32[]{:S(2)}) async-start(), calls=%async_computation.36 | async-start | bytes 122880 | tf_op jit(solution)/shard_map/reduce_scatter | solution.py:307
  1075.3 275.0 %reduce-scatter.40.cloned.1.call-start = ((), (), s32[]{:S(2)}) async-start(), calls=%async_computation.35 | async-start | bytes 122880 | tf_op jit(solution)/shard_map/reduce_scatter | solution.py:301
  1076.5 296.5 %reduce-scatter.38.cloned.1.call-start = ((), (), s32[]{:S(2)}) async-start(), calls=%async_computation.34 | async-start | bytes 737280 | tf_op jit(solution)/shard_map/reduce_scatter | solution.py:295
  1086.4 313.3 %reduce-scatter.36.cloned.1.call-start = ((), (), s32[]{:S(2)}) async-start(), calls=%async_computation.33 | async-start | bytes 2359296 | tf_op jit(solution)/shard_map/reduce_scatter | solution.py:68
  (38 other events, 1045.7 us)
Sparse Core Ops, SparseCore 0:
  96.2 42.4 reduce-scatter.17
  157.5 19.8 all-gather.9
  181.1 26.1 reduce-scatter.19
  300.5 140.8 reduce-scatter.25
  443.9 251.2 reduce-scatter.21
  703.1 62.7 all-gather.17
  767.4 62.7 all-gather.19
  831.8 62.7 all-gather.15
  897.3 26.1 reduce-scatter.27
  926.2 26.1 reduce-scatter.23
  970.4 37.9 reduce-scatter.29
  1014.6 21.6 reduce-scatter.33
  1039.4 21.6 reduce-scatter.31
  1063.0 20.0 all-gather.21
  1085.8 22.1 reduce-scatter.43
  1110.2 63.3 reduce-scatter.47
  1175.8 65.0 reduce-scatter.45
  1243.1 65.0 reduce-scatter.49
  1310.5 19.5 reduce-scatter.41
  1332.7 17.5 reduce-scatter.39
  1352.6 20.2 reduce-scatter.37
  1375.2 24.4 reduce-scatter.35
Sparse Core Ops, SparseCore 1:
  183.0 115.0 all-gather.11
  299.5 65.4 all-gather.13
